TPU v7x, 32 devices: a whole 2x2x4 slice. The times are simulated.
32 devices in a mesh: dp: 4 (over y, x), tensor: 8 (over z, core).
Axes of the slice: x: 2, y: 2, z: 4, core: 2. Of those that a mesh axis runs over, the one named last changes fastest.
Arguments:
- tokens: bfloat16 [768, 4096], P(('dp', 'tensor')), may hold values from -6 to 6
- out_grad: bfloat16 [768, 4096], P(('dp', 'tensor')), may hold values from -6 to 6
- w_gate: bfloat16 [4096, 14336], P(None, 'tensor'), may hold values from -0.09375 to 0.09375
- w_up: bfloat16 [4096, 14336], P(None, 'tensor'), may hold values from -0.09375 to 0.09375
- w_down: bfloat16 [14336, 4096], P('tensor'), may hold values from -0.046875 to 0.046875
Outputs:
- grad_tokens: bfloat16 [768, 4096], P(('dp', 'tensor'))
- grad_gate: bfloat16 [4096, 14336], P('dp', 'tensor')
- grad_up: bfloat16 [4096, 14336], P('dp', 'tensor')
- grad_down: bfloat16 [14336, 4096], P('tensor', 'dp')
All inputs are finite; a program needn't handle non-finite values.
Results may differ from a plain program's by a relative error of at most 0.014.
Values may be sent and summed in bfloat16 or wider, within the bound.
A program may use at most 128 MiB of HBM per device.

v0:
```python
import jax
import jax.numpy as jnp
from jax import lax
from jax.sharding import PartitionSpec as P


def contract_last(left, right):
    return lax.dot_general(
        left, right, (((1,), (1,)), ((), ())), preferred_element_type=jnp.float32
    )


def group_total(partials):
    rounded = partials.astype(jnp.bfloat16)
    rounded = lax.optimization_barrier(rounded)
    return jnp.sum(rounded.astype(jnp.float32), axis=0)


def per_device(tokens, out_grad, w_gate, w_up, w_down):
    group_tokens, group_grads = (
        lax.all_gather(tokens, "tensor", axis=0, tiled=True),
        lax.all_gather(out_grad, "tensor", axis=0, tiled=True),
    )
    gate_val = jnp.dot(group_tokens, w_gate, preferred_element_type=jnp.float32)
    up_val = jnp.dot(group_tokens, w_up, preferred_element_type=jnp.float32)
    sigmoid_gate = jax.nn.sigmoid(gate_val)
    act_val = gate_val * sigmoid_gate
    hidden = (act_val * up_val).astype(jnp.bfloat16)
    grad_hidden = contract_last(group_grads, w_down)
    grad_gate_pre = (
        grad_hidden * up_val * sigmoid_gate * (1.0 + gate_val * (1.0 - sigmoid_gate))
    ).astype(jnp.bfloat16)
    grad_up_pre = (grad_hidden * act_val).astype(jnp.bfloat16)
    grad_tokens = lax.psum_scatter(
        (contract_last(grad_gate_pre, w_gate) + contract_last(grad_up_pre, w_up)).astype(
            jnp.bfloat16
        ),
        "tensor",
        scatter_dimension=0,
        tiled=True,
    )
    groups = lax.axis_size("dp")
    group_rows = group_tokens.shape[0]
    tok_cols, grad_cols = (
        lax.all_to_all(group_tokens, "dp", split_axis=1, concat_axis=0, tiled=True),
        lax.all_to_all(group_grads, "dp", split_axis=1, concat_axis=0, tiled=True),
    )
    hid_all, gate_all, up_all = (
        lax.all_gather(hidden, "dp", axis=0, tiled=True),
        lax.all_gather(grad_gate_pre, "dp", axis=0, tiled=True),
        lax.all_gather(grad_up_pre, "dp", axis=0, tiled=True),
    )
    tok_split = tok_cols.reshape(groups, group_rows, -1)
    grad_split = grad_cols.reshape(groups, group_rows, -1)
    hid_split = hid_all.reshape(groups, group_rows, -1)
    gate_split = gate_all.reshape(groups, group_rows, -1)
    up_split = up_all.reshape(groups, group_rows, -1)
    sum_gate = group_total(
        jnp.einsum("gtd,gth->gdh", tok_split, gate_split, preferred_element_type=jnp.float32)
    )
    sum_up = group_total(
        jnp.einsum("gtd,gth->gdh", tok_split, up_split, preferred_element_type=jnp.float32)
    )
    sum_down = group_total(
        jnp.einsum("gth,gtd->ghd", hid_split, grad_split, preferred_element_type=jnp.float32)
    )
    return (
        grad_tokens,
        sum_gate.astype(jnp.bfloat16),
        sum_up.astype(jnp.bfloat16),
        sum_down.astype(jnp.bfloat16),
    )


def solution(mesh):
    in_specs = (
        P(("dp", "tensor"), None),
        P(("dp", "tensor"), None),
        P(None, "tensor"),
        P(None, "tensor"),
        P("tensor", None),
    )
    out_specs = (P(("dp", "tensor"), None), P("dp", "tensor"), P("dp", "tensor"), P("tensor", "dp"))
    return jax.shard_map(
        per_device, mesh=mesh, in_specs=in_specs, out_specs=out_specs, check_vma=False
    )
```

profile of v0, /device:TPU:0, one launch (start us, length us, event | category | flops | bytes accessed | tf_op | source)
XLA Modules:
  0.0 276.6 jit_solution(235035646883662496)
XLA Ops:
  7.2 0.0 all-gather.6.cloned.1.call-start
  7.2 0.7 all-gather.6.cloned.1.call-update
  7.9 0.0 all-gather.8.cloned.1.call-start
  7.9 0.7 all-gather.8.cloned.1.call-update
  8.6 0.0 all-gather.14.cloned.1.call-start
  8.7 28.9 %all-gather.6.cloned.1.call-done = bf16[192,4096]{1,0:T(8,128)(2,1)} async-done(((bf16[24,4096]{1,0:T(8,128)(2,1)}), bf16[192,4096]{1,0:T(8,128)(2,1)}) %all-gather.6.cloned.1.call-update) | async-done | bytes 1572880 | tf_op jit(solution)/shard_map/all_gather | solution.py:22
  37.6 8.6 %fusion.5 = f32[192,1792]{1,0:T(8,128)S(1)} fusion(bf16[192,4096]{1,0:T(8,128)(2,1)} %all-gather.6.cloned.1.call-done, bf16[1792,4096]{1,0:T(8,128)(2,1)} %param.9), kind=kOutput, calls=%fused_computation.15 | convolution fusion | flops 2818572288 | bytes 17629184 | tf_op jit(solution)/shard_map/dot_general | solution.py:8
  46.3 17.4 %all-gather.8.cloned.1.call-done = bf16[192,4096]{1,0:T(8,128)(2,1)} async-done(((bf16[24,4096]{1,0:T(8,128)(2,1)}), bf16[192,4096]{1,0:T(8,128)(2,1)}) %all-gather.8.cloned.1.call-update) | async-done | bytes 1572880 | tf_op jit(solution)/shard_map/all_gather | solution.py:21
  63.7 0.0 copy-start.1
  63.7 0.0 copy-start.4
  63.7 9.3 %fusion.6 = f32[192,1792]{1,0:T(8,128)S(1)} fusion(bf16[192,4096]{1,0:T(8,128)(2,1)} %all-gather.8.cloned.1.call-done, bf16[4096,1792]{1,0:T(8,128)(2,1)} %param.7), kind=kOutput, calls=%fused_computation.16 | convolution fusion | flops 2818572288 | bytes 17629184 | tf_op jit(solution)/shard_map/dot_general | solution.py:24
  73.0 0.0 copy-done.1
  73.0 1.0 copy-done.4
  74.0 4.8 %multiply_convert_fusion = (bf16[192,1792]{1,0:T(8,128)(2,1)}, bf16[192,1792]{1,0:T(8,128)(2,1)}, bf16[192,1792]{1,0:T(8,128)(2,1)}) fusion(f32[192,1792]{1,0:T(8,128)S(1)} %fusion.6, f32[192,1792]{1,0:T(8,128)S(1)} %fusion.5, bf16[192,4096]{1,0:T(8,128)(2,1)S(1)} %copy-done.1, bf16[4096,1792]{1,0:T(8,128)(2,1)S(1)} %copy-done.4), kind=kOutput, calls=%fused_computation.10 | convolution fusion | flops 2823733248 | bytes 21069824 | tf_op jit(solution)/shard_map/dot_general | solution.py:25
  78.7 0.0 copy-start
  78.7 0.0 all-gather.14.cloned.1.call-update
  78.8 0.0 all-gather.12.cloned.1.call-start
  78.8 0.5 all-gather.12.cloned.1.call-update
  79.4 0.0 all-gather.10.cloned.1.call-start
  79.4 0.5 all-gather.10.cloned.1.call-update
  79.9 0.2 copy-done
  80.2 1.3 copy.19
  81.5 0.0 copy-start.2
  81.5 3.8 %all-to-all-start.1 = ((bf16[192,4,1024]{2,0,1:T(8,128)(2,1)}), bf16[192,4,1024]{2,0,1:T(8,128)(2,1)S(1)}, u32[]{:S(2)}, u32[]{:S(2)}) async-start(bf16[192,4,1024]{2,0,1:T(8,128)(2,1)} %bitcast.34), calls=%async_computation.2 | async-start | bytes 3145728 | tf_op jit(solution)/shard_map/all_to_all | solution.py:46
  85.2 0.0 copy-start.3
  85.2 0.0 copy-done.2
  85.2 1.3 copy.20
  86.5 0.0 copy-done.3
  86.6 11.7 %fusion.7 = f32[192,4096]{1,0:T(8,128)} fusion(bf16[192,1792]{1,0:T(8,128)(2,1)S(1)} %copy-done.3, bf16[4096,1792]{1,0:T(8,128)(2,1)} %param.7), kind=kOutput, calls=%fused_computation.17 | convolution fusion | flops 2818572288 | bytes 18513920 | tf_op jit(solution)/shard_map/dot_general | solution.py:8
  98.3 14.1 %all-to-all-done.1 = bf16[192,4,1024]{2,0,1:T(8,128)(2,1)S(1)} async-done(((bf16[192,4,1024]{2,0,1:T(8,128)(2,1)}), bf16[192,4,1024]{2,0,1:T(8,128)(2,1)S(1)}, u32[]{:S(2)}, u32[]{:S(2)}) %all-to-all-start.1) | async-done | bytes 1572896 | tf_op jit(solution)/shard_map/all_to_all | solution.py:46
  112.4 3.6 %all-to-all-start = ((bf16[192,4,1024]{2,0,1:T(8,128)(2,1)}), bf16[192,4,1024]{2,0,1:T(8,128)(2,1)S(1)}, u32[]{:S(2)}, u32[]{:S(2)}) async-start(bf16[192,4,1024]{2,0,1:T(8,128)(2,1)} %bitcast.36), calls=%async_computation.1 | async-start | bytes 3145728 | tf_op jit(solution)/shard_map/all_to_all | solution.py:45
  116.0 0.2 reduce-scatter.2.cloned.1.call-start
  116.2 12.3 %fusion = bf16[192,4096]{1,0:T(8,128)(2,1)} fusion(f32[192,4096]{1,0:T(8,128)} %fusion.7, bf16[192,1792]{1,0:T(8,128)(2,1)} %get-tuple-element.10, bf16[4096,1792]{1,0:T(8,128)(2,1)} %param.8), kind=kOutput, calls=%fused_computation.4 | convolution fusion | flops 2820145152 | bytes 20086784 | tf_op jit(solution)/shard_map/dot_general | solution.py:8
  128.5 0.0 reduce-scatter.2.cloned.1.call-update
  128.5 21.5 %all-gather.14.cloned.1.call-done = bf16[768,1792]{1,0:T(8,128)(2,1)} async-done(((bf16[192,1792]{1,0:T(8,128)(2,1)}), bf16[768,1792]{1,0:T(8,128)(2,1)}) %all-gather.14.cloned.1.call-update) | async-done | bytes 2752528 | tf_op jit(solution)/shard_map/all_gather | solution.py:49
  150.1 9.4 %convolution_convert_fusion = bf16[4,1792,1024]{2,1,0:T(8,128)(2,1)} fusion(bf16[4,192,1792]{2,1,0:T(8,128)(2,1)} %bitcast.39, bf16[192,4,1024]{2,0,1:T(8,128)(2,1)S(1)} %all-to-all-done.1), kind=kOutput, calls=%fused_computation.2 | convolution fusion | flops 2825912320 | bytes 19005440 | tf_op jit(solution)/shard_map/gth,gtd->ghd/dot_general | solution.py:65
  159.5 0.0 all-to-all-done
  159.5 31.0 %all-gather.12.cloned.1.call-done = bf16[768,1792]{1,0:T(8,128)(2,1)} async-done(((bf16[192,1792]{1,0:T(8,128)(2,1)}), bf16[768,1792]{1,0:T(8,128)(2,1)}) %all-gather.12.cloned.1.call-update) | async-done | bytes 2752528 | tf_op jit(solution)/shard_map/all_gather | solution.py:51
  190.5 9.5 %convert_bitcast_fusion = bf16[4,1024,1792]{1,2,0:T(8,128)(2,1)} fusion(bf16[4,192,1792]{2,1,0:T(8,128)(2,1)} %bitcast.38, bf16[192,4,1024]{2,0,1:T(8,128)(2,1)S(1)} %all-to-all-done), kind=kOutput, calls=%fused_computation | convolution fusion | flops 2825912320 | bytes 19005440 | tf_op jit(solution)/shard_map/gtd,gth->gdh/dot_general | solution.py:62
  200.0 11.1 %reduce_sum.38 = bf16[1792,1024]{1,0:T(8,128)(2,1)} reduce(bf16[4,1792,1024]{2,1,0:T(8,128)(2,1)} %convolution_convert_fusion, bf16[]{:T(256)} %constant.6.clone.1), dimensions={0}, to_apply=%region_3.0 | reduce | flops 5505024 | bytes 18350082 | tf_op jit(solution)/shard_map/reduce_sum | solution.py:16
  211.1 11.1 %reduce_sum.37 = bf16[1024,1792]{0,1:T(8,128)(2,1)} reduce(bf16[4,1024,1792]{1,2,0:T(8,128)(2,1)} %convert_bitcast_fusion, bf16[]{:T(256)} %constant.6.clone.1), dimensions={0}, to_apply=%region_2.0 | reduce | flops 5505024 | bytes 18350082 | tf_op jit(solution)/shard_map/reduce_sum | solution.py:16
  222.1 5.9 %copy.14 = bf16[1024,1792]{1,0:T(8,128)(2,1)} copy(bf16[1024,1792]{0,1:T(8,128)(2,1)} %reduce_sum.37) | data formatting | bytes 7340032
  228.1 4.8 %all-gather.10.cloned.1.call-done = bf16[768,1792]{1,0:T(8,128)(2,1)} async-done(((bf16[192,1792]{1,0:T(8,128)(2,1)}), bf16[768,1792]{1,0:T(8,128)(2,1)}) %all-gather.10.cloned.1.call-update) | async-done | bytes 2752528 | tf_op jit(solution)/shard_map/all_gather | solution.py:50
  232.8 9.4 %convert_bitcast_fusion.1 = bf16[4,1024,1792]{1,2,0:T(8,128)(2,1)} fusion(bf16[4,192,1792]{2,1,0:T(8,128)(2,1)} %bitcast.37, bf16[192,4,1024]{2,0,1:T(8,128)(2,1)S(1)} %all-to-all-done), kind=kOutput, calls=%fused_computation.1 | convolution fusion | flops 2825912320 | bytes 19005440 | tf_op jit(solution)/shard_map/gtd,gth->gdh/dot_general | solution.py:59
  242.2 11.0 %reduce_sum.36 = bf16[1024,1792]{0,1:T(8,128)(2,1)} reduce(bf16[4,1024,1792]{1,2,0:T(8,128)(2,1)} %convert_bitcast_fusion.1, bf16[]{:T(256)} %constant.6.clone.1), dimensions={0}, to_apply=%region_1.0 | reduce | flops 5505024 | bytes 18350082 | tf_op jit(solution)/shard_map/reduce_sum | solution.py:16
  253.2 5.9 %copy.13 = bf16[1024,1792]{1,0:T(8,128)(2,1)} copy(bf16[1024,1792]{0,1:T(8,128)(2,1)} %reduce_sum.36) | data formatting | bytes 7340032
  259.1 10.6 %reduce-scatter.2.cloned.1.call-done = bf16[24,4096]{1,0:T(8,128)(2,1)} async-done(((bf16[192,4096]{1,0:T(8,128)(2,1)}), bf16[24,4096]{1,0:T(8,128)(2,1)}) %reduce-scatter.2.cloned.1.call-update) | async-done | bytes 196624 | tf_op jit(solution)/shard_map/reduce_scatter | solution.py:34
Async XLA Ops:
  7.2 30.5 %all-gather.6.cloned.1.call-start = ((), (), s32[]{:S(2)}) async-start(), calls=%async_computation.3 | async-start | bytes 1769472 | tf_op jit(solution)/shard_map/all_gather | solution.py:22
  7.9 55.8 %all-gather.8.cloned.1.call-start = ((), (), s32[]{:S(2)}) async-start(), calls=%async_computation.4 | async-start | bytes 1769472 | tf_op jit(solution)/shard_map/all_gather | solution.py:21
  8.6 141.4 %all-gather.14.cloned.1.call-start = ((), (), s32[]{:S(2)}) async-start(), calls=%async_computation.8 | async-start | bytes 3440640 | tf_op jit(solution)/shard_map/all_gather | solution.py:49
  63.7 9.3 %copy-start.1 = (bf16[192,4096]{1,0:T(8,128)(2,1)S(1)}, bf16[192,4096]{1,0:T(8,128)(2,1)}, u32[]{:S(2)}) copy-start(bf16[192,4096]{1,0:T(8,128)(2,1)} %all-gather.8.cloned.1.call-done) | copy-start | bytes 4718596
  63.7 10.3 %copy-start.4 = (bf16[4096,1792]{1,0:T(8,128)(2,1)S(1)}, bf16[4096,1792]{1,0:T(8,128)(2,1)}, u32[]{:S(2)}) copy-start(bf16[4096,1792]{1,0:T(8,128)(2,1)} %param.8) | copy-start | bytes 44040196
  78.7 1.4 copy-start
  78.8 111.8 %all-gather.12.cloned.1.call-start = ((), (), s32[]{:S(2)}) async-start(), calls=%async_computation.7 | async-start | bytes 3440640 | tf_op jit(solution)/shard_map/all_gather | solution.py:51
  79.4 153.5 %all-gather.10.cloned.1.call-start = ((), (), s32[]{:S(2)}) async-start(), calls=%async_computation.6 | async-start | bytes 3440640 | tf_op jit(solution)/shard_map/all_gather | solution.py:50
  81.5 3.8 %copy-start.2 = (bf16[192,4096]{1,0:T(8,128)(2,1)S(1)}, bf16[192,4096]{1,0:T(8,128)(2,1)}, u32[]{:S(2)}) copy-start(bf16[192,4096]{1,0:T(8,128)(2,1)} %all-gather.8.cloned.1.call-done) | copy-start | bytes 4718596
  81.5 30.9 %all-to-all-start.1 = ((bf16[192,4,1024]{2,0,1:T(8,128)(2,1)}), bf16[192,4,1024]{2,0,1:T(8,128)(2,1)S(1)}, u32[]{:S(2)}, u32[]{:S(2)}) async-start(bf16[192,4,1024]{2,0,1:T(8,128)(2,1)} %bitcast.34), calls=%async_computation.2 | async-start | bytes 3145728 | tf_op jit(solution)/shard_map/all_to_all | solution.py:46
  85.2 1.3 copy-start.3
  112.4 47.1 %all-to-all-start = ((bf16[192,4,1024]{2,0,1:T(8,128)(2,1)}), bf16[192,4,1024]{2,0,1:T(8,128)(2,1)S(1)}, u32[]{:S(2)}, u32[]{:S(2)}) async-start(bf16[192,4,1024]{2,0,1:T(8,128)(2,1)} %bitcast.36), calls=%async_computation.1 | async-start | bytes 3145728 | tf_op jit(solution)/shard_map/all_to_all | solution.py:45
  116.0 153.8 %reduce-scatter.2.cloned.1.call-start = ((), (), s32[]{:S(2)}) async-start(), calls=%async_computation.5 | async-start | bytes 1769472 | tf_op jit(solution)/shard_map/reduce_scatter | solution.py:34
Sparse Core Ops, SparseCore 0:
  9.6 27.9 all-gather.5
  39.3 24.3 all-gather.7
  78.9 71.1 all-gather.13
  151.7 38.7 all-gather.11
  192.2 40.5 all-gather.9
  235.6 34.0 reduce-scatter.1
where the time goes:
time: 277 us
  waiting for transfers between devices  131 us (47%)
  matrix products  75 us (27%)
  other arithmetic  33.1 us (12%)
  local copies, waits for them, and re-layouts  15.7 us (6%)
  between operations  14.2 us (5%)
  starting transfers between devices  7.77 us (3%)
    reduce_sum x3, other arithmetic, group_total(): return jnp.sum(rounded.astype(jnp.float32), axis=0)  33.1 us
    dot_general x3, matrix products, contract_last(): lax.dot_general(left, right, (((1,), (1,)), ((), ())), preferred_element_...  32.7 us
    all_gather x1, waiting for transfers between devices, per_device(): lax.all_gather(grad_up_pre, 'dp', axis=0, tiled=True)  31 us
    all_gather x1, waiting for transfers between devices, per_device(): lax.all_gather(out_grad, 'tensor', axis=0, tiled=True)  28.9 us
    all_gather x1, waiting for transfers between devices, per_device(): lax.all_gather(hidden, 'dp', axis=0, tiled=True)  21.5 us
    all_gather x1, waiting for transfers between devices, per_device(): lax.all_gather(tokens, 'tensor', axis=0, tiled=True)  17.4 us
    all_to_all x1, waiting for transfers between devices, per_device(): lax.all_to_all(group_grads, 'dp', split_axis=1, concat_axis=0, tiled=True)  14.1 us
    unnamed x12, local copies, waits for them, and re-layouts  13.1 us
  transfers between devices with their start and end apart: 8, of which 7 were waited for; matrix products, arithmetic and copies ran while one was open for 39% of the time, Pallas kernels for 0%

commit v1 on v0

v1 whole, which is shorter than its diff:
```python
import functools

import jax
import jax.numpy as jnp
from jax import lax
from jax.experimental import pallas as pl
from jax.experimental.pallas import tpu as pltpu
from jax.sharding import PartitionSpec as P

MESH = pl.DeviceIdType.MESH


def lookup(index, table):
    value = jnp.int32(table[0])
    for k in range(1, len(table)):
        value = jnp.where(index == k, jnp.int32(table[k]), value)
    return value


def ring_order(n):
    return [p ^ (p >> 1) for p in range(n)] if n & (n - 1) == 0 else list(range(n))


def position(n_tensor):
    group, slot = lax.axis_index("dp"), lax.axis_index("tensor")
    return group, slot, slot // 2, slot % 2, n_tensor // 2


def gather_kernel(
    n_dp, n_tensor, tok, grad, out_tok, out_grad,
    line_send, line_recv, ring_send, ring_recv, pair_send, pair_recv, own_sem,
):
    group, slot, level, core, n_levels = position(n_tensor)
    order = ring_order(n_dp)
    where = {g: p for p, g in enumerate(order)}
    half = n_dp // 2

    def at_distance(s):
        return lookup(group, [order[(where[g] + s) % n_dp] for g in range(n_dp)])

    neighbours = (at_distance(1), at_distance(-1))
    origin = [[at_distance(-s) for s in range(half + 1)], [at_distance(s) for s in range(half + 1)]]
    partner = (group, level * 2 + 1 - core)
    ins, outs = (tok, grad), (out_tok, out_grad)

    def level_slot(k):
        return lax.rem(level + k + n_levels, n_levels) * 2 + core

    barrier = pltpu.get_barrier_semaphore()
    peers = [(group, level_slot(k)) for k in range(1, n_levels)]
    peers += [(neighbours[0], slot), (neighbours[1], slot), partner]
    for peer in peers:
        pl.semaphore_signal(barrier, inc=1, device_id=peer, device_id_type=MESH)
    pl.semaphore_wait(barrier, len(peers))

    started = []

    def send(src, dst, send_sem, recv_sem, peer):
        copy = pltpu.make_async_remote_copy(
            src_ref=src, dst_ref=dst, send_sem=send_sem, recv_sem=recv_sem,
            device_id=peer, device_id_type=MESH,
        )
        copy.start()
        started.append(copy)

    def arrived(ref, send_sem, recv_sem):
        pltpu.make_async_remote_copy(
            src_ref=ref, dst_ref=ref, send_sem=send_sem, recv_sem=recv_sem,
            device_id=partner, device_id_type=MESH,
        ).wait_recv()

    shared = []

    def share(src, ref, a, number):
        send(src, ref, pair_send.at[a, number], pair_recv.at[a, number], partner)

    def pair_slot(u):
        return lax.rem(level - u + n_levels, n_levels) * 2 + 1 - core

    def process_ring(u):
        spot = level_slot(-u)
        for s in range(1, half + 1):
            for direction in (0, 1):
                for a in (0, 1):
                    if s == half and a != direction:
                        continue
                    source = origin[direction][s]
                    ref = outs[a].at[source, spot]
                    arrived(ref, ring_send.at[u, s, direction, a], ring_recv.at[u, s, direction, a])
                    onward = s + 1
                    if onward < half or (onward == half and a == direction):
                        send(ref, ref, ring_send.at[u, onward, direction, a],
                             ring_recv.at[u, onward, direction, a], (neighbours[direction], slot))
                    number = u * n_dp + (s if direction == 0 else n_dp - s)
                    if s == half:
                        number = u * n_dp + half
                    share(ref, ref, a, number)
                    shared.append((a, number, source, pair_slot(u)))

    for direction in (0, 1):
        for a in (0, 1):
            if half > 1 or a == direction:
                send(ins[a], outs[a].at[group, slot], ring_send.at[0, 1, direction, a],
                     ring_recv.at[0, 1, direction, a], (neighbours[direction], slot))
    for k in range(1, n_levels):
        for a in (0, 1):
            send(ins[a], outs[a].at[group, slot], line_send.at[k, a], line_recv.at[k, a],
                 (group, level_slot(k)))
    own = []
    for a in (0, 1):
        share(ins[a], outs[a].at[group, slot], a, 0)
        shared.append((a, 0, group, pair_slot(0)))
        copy = pltpu.make_async_copy(ins[a], outs[a].at[group, slot], own_sem.at[a])
        copy.start()
        own.append(copy)

    for u in range(1, n_levels):
        process_ring(u - 1)
        spot = level_slot(-u)
        for a in (0, 1):
            ref = outs[a].at[group, spot]
            arrived(ref, line_send.at[u, a], line_recv.at[u, a])
            for direction in (0, 1):
                if half > 1 or a == direction:
                    send(ref, ref, ring_send.at[u, 1, direction, a],
                         ring_recv.at[u, 1, direction, a], (neighbours[direction], slot))
            share(ref, ref, a, u * n_dp)
            shared.append((a, u * n_dp, group, pair_slot(u)))
    process_ring(n_levels - 1)

    for a, number, source, spot in shared:
        arrived(outs[a].at[source, spot], pair_send.at[a, number], pair_recv.at[a, number])
    for copy in started:
        copy.wait_send()
    for copy in own:
        copy.wait()


def gather_tokens(tokens, out_grad, n_dp, n_tensor):
    rows, width = tokens.shape
    n_levels, half = n_tensor // 2, n_dp // 2
    full = jax.ShapeDtypeStruct((n_dp, n_tensor, rows, width), tokens.dtype)
    dma = pltpu.SemaphoreType.DMA
    anywhere = pl.BlockSpec(memory_space=pl.ANY)
    tok, grad = pl.pallas_call(
        functools.partial(gather_kernel, n_dp, n_tensor),
        out_shape=(full, full),
        in_specs=[anywhere] * 2,
        out_specs=(anywhere, anywhere),
        scratch_shapes=[
            dma((n_levels, 2)), dma((n_levels, 2)),
            dma((n_levels, half + 1, 2, 2)), dma((n_levels, half + 1, 2, 2)),
            dma((2, n_levels * n_dp)), dma((2, n_levels * n_dp)),
            dma((2,)),
        ],
        compiler_params=pltpu.CompilerParams(collective_id=0, has_side_effects=True),
        name="gather_tokens",
    )(tokens, out_grad)
    return tok.reshape(-1, width), grad.reshape(-1, width)


def scatter_kernel(
    n_tensor, part, out, mine, theirs, summed, landed,
    mine_sem, pair_send, pair_recv, line_send, line_recv,
):
    group, slot, level, core, n_levels = position(n_tensor)
    partner = (group, level * 2 + 1 - core)

    def other(k):
        return lax.rem(level + k, n_levels)

    barrier = pltpu.get_barrier_semaphore()
    peers = [(group, other(k) * 2 + core) for k in range(1, n_levels)] + [partner]
    for peer in peers:
        pl.semaphore_signal(barrier, inc=1, device_id=peer, device_id_type=MESH)
    local = []
    for k in range(n_levels):
        copy = pltpu.make_async_copy(part.at[other(k) * 2 + core], mine.at[k], mine_sem.at[k])
        copy.start()
        local.append(copy)
    pl.semaphore_wait(barrier, len(peers))

    pair = []
    for k in [*range(1, n_levels), 0]:
        copy = pltpu.make_async_remote_copy(
            src_ref=part.at[other(k) * 2 + 1 - core], dst_ref=theirs.at[k],
            send_sem=pair_send.at[k], recv_sem=pair_recv.at[k],
            device_id=partner, device_id_type=MESH,
        )
        copy.start()
        pair.append((k, copy))
    for k, copy in pair:
        local[k].wait()
        copy.wait_recv()
        if k > 0:
            summed[k] = (mine[k].astype(jnp.float32) + theirs[k].astype(jnp.float32)).astype(summed.dtype)
    line = []
    for k in range(1, n_levels):
        copy = pltpu.make_async_remote_copy(
            src_ref=summed.at[k], dst_ref=landed.at[k],
            send_sem=line_send.at[k], recv_sem=line_recv.at[k],
            device_id=(group, other(k) * 2 + core), device_id_type=MESH,
        )
        copy.start()
        line.append(copy)
    total = mine[0].astype(jnp.float32) + theirs[0].astype(jnp.float32)
    for k in range(1, n_levels):
        line[k - 1].wait_recv()
        total = total + landed[k].astype(jnp.float32)
    out[...] = total.astype(out.dtype)
    for k, copy in pair:
        copy.wait_send()
    for copy in line:
        copy.wait_send()


def scatter_sum(part, n_tensor):
    rows, width = part.shape[0] // n_tensor, part.shape[1]
    n_levels = n_tensor // 2
    dma = pltpu.SemaphoreType.DMA
    block = pltpu.VMEM((n_levels, rows, width), part.dtype)
    return pl.pallas_call(
        functools.partial(scatter_kernel, n_tensor),
        out_shape=jax.ShapeDtypeStruct((rows, width), part.dtype),
        in_specs=[pl.BlockSpec(memory_space=pl.ANY)],
        out_specs=pl.BlockSpec(memory_space=pltpu.VMEM),
        scratch_shapes=[block] * 4 + [dma((n_levels,))] * 5,
        compiler_params=pltpu.CompilerParams(collective_id=1, has_side_effects=True),
        name="scatter_sum",
    )(part.reshape(n_tensor, rows, width))


def contract(left, right, dims):
    return lax.dot_general(left, right, (dims, ((), ())), preferred_element_type=jnp.float32)


def per_device(n_dp, n_tensor, tokens, out_grad, w_gate, w_up, w_down):
    tok, grad = gather_tokens(tokens, out_grad, n_dp, n_tensor)
    group = lax.axis_index("dp")
    rows, columns = tok.shape[0] // n_dp, tok.shape[1] // n_dp
    gate_val = contract(tok, w_gate, ((1,), (0,)))
    up_val = contract(tok, w_up, ((1,), (0,)))
    grad_hidden = contract(grad, w_down, ((1,), (1,)))
    sigmoid_gate = jax.nn.sigmoid(gate_val)
    act_val = gate_val * sigmoid_gate
    hidden = (act_val * up_val).astype(jnp.bfloat16)
    gate_pre = (
        grad_hidden * up_val * sigmoid_gate * (1.0 + gate_val * (1.0 - sigmoid_gate))
    ).astype(jnp.bfloat16)
    up_pre = (grad_hidden * act_val).astype(jnp.bfloat16)
    hidden, gate_pre, up_pre = lax.optimization_barrier((hidden, gate_pre, up_pre))
    own_gate = lax.dynamic_slice_in_dim(gate_pre, group * rows, rows, 0)
    own_up = lax.dynamic_slice_in_dim(up_pre, group * rows, rows, 0)
    part = (
        contract(own_gate, w_gate, ((1,), (1,))) + contract(own_up, w_up, ((1,), (1,)))
    ).astype(jnp.bfloat16)
    grad_tokens = scatter_sum(part, n_tensor)
    tok_cols = lax.dynamic_slice_in_dim(tok, group * columns, columns, 1)
    grad_cols = lax.dynamic_slice_in_dim(grad, group * columns, columns, 1)
    return (
        grad_tokens,
        contract(tok_cols, gate_pre, ((0,), (0,))).astype(jnp.bfloat16),
        contract(tok_cols, up_pre, ((0,), (0,))).astype(jnp.bfloat16),
        contract(hidden, grad_cols, ((0,), (0,))).astype(jnp.bfloat16),
    )


def solution(mesh):
    n_dp, n_tensor = mesh.shape["dp"], mesh.shape["tensor"]
    in_specs = (
        P(("dp", "tensor"), None),
        P(("dp", "tensor"), None),
        P(None, "tensor"),
        P(None, "tensor"),
        P("tensor", None),
    )
    out_specs = (P(("dp", "tensor"), None), P("dp", "tensor"), P("dp", "tensor"), P("tensor", "dp"))
    return jax.shard_map(
        functools.partial(per_device, n_dp, n_tensor),
        mesh=mesh, in_specs=in_specs, out_specs=out_specs, check_vma=False,
    )
```

time: 277 us -> 197 us (0.71)
  waiting for transfers between devices: 131 us -> 0 us
  Pallas kernels: 0 us -> 97.1 us
  other arithmetic: 33.1 us -> 0 us
  matrix products: 75 us -> 96.3 us
  local copies, waits for them, and re-layouts: 15.7 us -> 1.63 us
  between operations: 14.2 us -> 0.68 us
  starting transfers between devices: 7.77 us -> 0 us
    all_gather x5 -> x0, waiting for transfers between devices: 104 us -> none  [the longest x1 31 us: per_device(): lax.all_gather(grad_up_pre, 'dp', axis=0, tiled=True)]
    pallas_call x0 -> x2, Pallas kernels: none -> 97.1 us  [the longest x1 72.6 us: gather_tokens(): pl.pallas_call(functools.partial(gather_kernel, n_dp, n_tensor), out_shap...]
    reduce_sum x3 -> x0, other arithmetic: 33.1 us -> none  [group_total(): return jnp.sum(rounded.astype(jnp.float32), axis=0)]
    dot_general x8, matrix products: 75 us -> 96.3 us  [contract(): lax.dot_general(left, right, (dims, ((), ())), preferred_element_type=jnp...]
    all_to_all x2 -> x0, waiting for transfers between devices: 14.1 us -> none  [the longest x1 14.1 us: per_device(): lax.all_to_all(group_grads, 'dp', split_axis=1, concat_axis=0, tiled=True)]
    unnamed x12 -> x9, local copies, waits for them, and re-layouts: 13.1 us -> 1.63 us
    reduce_scatter x1 -> x0, waiting for transfers between devices: 10.6 us -> none  [per_device(): lax.psum_scatter((contract_last(grad_gate_pre, w_gate) + contract_last(gr...]
    all_to_all x2 -> x0, starting transfers between devices: 7.35 us -> none  [the longest x1 3.79 us: per_device(): lax.all_to_all(group_grads, 'dp', split_axis=1, concat_axis=0, tiled=True)]
  transfers between devices with their start and end apart: 8 -> 0, of which waited for: 7 -> 0; matrix products, arithmetic and copies ran while one was open for 39% -> 0% of each run, Pallas kernels for 0% -> 0%
where the time goes in v1:
time: 197 us; the launch traced here: 196 us
  Pallas kernels  97.1 us (49%)
  matrix products  96.3 us (49%)
    dot_general x8, matrix products, contract(): lax.dot_general(left, right, (dims, ((), ())), preferred_element_type=jnp...  96.3 us
    pallas_call x1, Pallas kernels, gather_tokens(): pl.pallas_call(functools.partial(gather_kernel, n_dp, n_tensor), out_shap...  72.6 us
    pallas_call x1, Pallas kernels, scatter_sum(): pl.pallas_call(functools.partial(scatter_kernel, n_tensor), out_shape=jax...  24.4 us

profile of v1, /device:TPU:0, one launch (start us, length us, event | category | flops | bytes accessed | tf_op | source)
XLA Modules:
  0.0 195.7 jit_solution(7342055347459197563)
XLA Ops:
  0.6 72.6 %gather_tokens.1 = (bf16[4,8,24,4096]{3,2,1,0:T(8,128)(2,1)}, bf16[4,8,24,4096]{3,2,1,0:T(8,128)(2,1)}) custom-call(bf16[24,4096]{1,0:T(8,128)(2,1)} %tok.1, bf16[24,4096]{1,0:T(8,128)(2,1)} %grad.1), custom_call_target="tpu_custom_call" | custom-call | tf_op jit(solution)/shard_map/gather_tokens/pallas_call | solution.py:145
  73.3 0.0 copy-start
  73.3 0.0 copy-start.1
  73.3 18.2 %fusion.13 = f32[768,1792]{1,0:T(8,128)} fusion(bf16[768,4096]{1,0:T(8,128)(2,1)} %bitcast.15, bf16[4096,1792]{1,0:T(8,128)(2,1)} %param.7), kind=kOutput, calls=%fused_computation.21 | convolution fusion | flops 11274289152 | bytes 26476544 | tf_op jit(solution)/shard_map/dot_general | solution.py:234
  91.5 0.0 copy-done
  91.5 0.0 copy-done.1
  91.5 13.3 %fusion.14 = f32[768,1792]{1,0:T(8,128)} fusion(bf16[768,4096]{1,0:T(8,128)(2,1)S(1)} %bitcast.18, bf16[4096,1792]{1,0:T(8,128)(2,1)S(1)} %copy-done), kind=kOutput, calls=%fused_computation.22 | convolution fusion | flops 11274289152 | bytes 26476544 | tf_op jit(solution)/shard_map/dot_general | solution.py:234
  104.8 24.1 %multiply_convert_fusion = (bf16[768,1792]{1,0:T(8,128)(2,1)S(1)}, bf16[768,1792]{1,0:T(8,128)(2,1)}, bf16[768,1792]{1,0:T(8,128)(2,1)}) fusion(f32[768,1792]{1,0:T(8,128)} %fusion.13, f32[768,1792]{1,0:T(8,128)} %fusion.14, bf16[768,4096]{1,0:T(8,128)(2,1)} %bitcast.19, bf16[1792,4096]{1,0:T(8,128)(2,1)} %param.9), kind=kOutput, calls=%fused_computation | convolution fusion | flops 11294932992 | bytes 40239104 | tf_op jit(solution)/shard_map/dot_general | solution.py:234
  128.8 0.0 copy-start.2
  128.9 8.1 %convolution_convert_fusion = bf16[1792,1024]{1,0:T(8,128)(2,1)} fusion(bf16[768,1792]{1,0:T(8,128)(2,1)} %get-tuple-element.13, bf16[768,4096]{1,0:T(8,128)(2,1)} %bitcast.20, s32[]{:T(128)S(6)} %select_n.9), kind=kOutput, calls=%fused_computation.7 | convolution fusion | flops 2820407296 | bytes 7995396 | tf_op jit(solution)/shard_map/dot_general | solution.py:234
  137.0 0.0 copy-done.2
  137.0 0.0 copy-start.3
  137.0 6.5 %convolution_convert_fusion.1 = bf16[1024,1792]{1,0:T(8,128)(2,1)} fusion(bf16[768,1792]{1,0:T(8,128)(2,1)S(1)} %get-tuple-element.12, bf16[768,4096]{1,0:T(8,128)(2,1)} %bitcast.16, s32[]{:T(128)S(6)} %select_n.9), kind=kOutput, calls=%fused_computation.8 | convolution fusion | flops 2820407296 | bytes 7995396 | tf_op jit(solution)/shard_map/dot_general | solution.py:234
  143.5 0.0 copy-done.3
  143.5 6.3 %convolution_convert_fusion.2 = bf16[1024,1792]{1,0:T(8,128)(2,1)} fusion(bf16[768,1792]{1,0:T(8,128)(2,1)S(1)} %copy-done.3, bf16[768,4096]{1,0:T(8,128)(2,1)} %bitcast.17, s32[]{:T(128)S(6)} %select_n.9), kind=kOutput, calls=%fused_computation.9 | convolution fusion | flops 2820407296 | bytes 7995396 | tf_op jit(solution)/shard_map/dot_general | solution.py:234
  149.8 8.4 %fusion.6 = f32[192,4096]{1,0:T(8,128)S(1)} fusion(bf16[4096,1792]{1,0:T(8,128)(2,1)} %param.7, bf16[768,1792]{1,0:T(8,128)(2,1)} %get-tuple-element.11, s32[]{:T(128)S(6)} %select_n.8), kind=kOutput, calls=%fused_computation.14 | convolution fusion | flops 2818572288 | bytes 18513924 | tf_op jit(solution)/shard_map/dot_general | solution.py:234
  158.2 11.5 %fusion.1 = bf16[192,4096]{1,0:T(8,128)(2,1)} fusion(f32[192,4096]{1,0:T(8,128)S(1)} %fusion.6, bf16[4096,1792]{1,0:T(8,128)(2,1)} %param.8, bf16[768,1792]{1,0:T(8,128)(2,1)} %copy-done.2, s32[]{:T(128)S(6)} %select_n.8), kind=kOutput, calls=%fused_computation.6 | convolution fusion | flops 2820145152 | bytes 20086788 | tf_op jit(solution)/shard_map/dot_general | solution.py:234
  169.7 24.4 %scatter_sum.1 = bf16[24,4096]{1,0:T(8,128)(2,1)} custom-call(bf16[8,24,4096]{2,1,0:T(8,128)(2,1)} %bitcast.14), custom_call_target="tpu_custom_call" | custom-call | tf_op jit(solution)/shard_map/scatter_sum/pallas_call | solution.py:222
  194.1 1.6 copy.10
Async XLA Ops:
  73.3 18.2 %copy-start = (bf16[4096,1792]{1,0:T(8,128)(2,1)S(1)}, bf16[4096,1792]{1,0:T(8,128)(2,1)}, u32[]{:S(2)}) copy-start(bf16[4096,1792]{1,0:T(8,128)(2,1)} %param.8) | copy-start | bytes 44040196
  73.3 18.2 %copy-start.1 = (bf16[4,8,24,4096]{3,2,1,0:T(8,128)(2,1)S(1)}, bf16[4,8,24,4096]{3,2,1,0:T(8,128)(2,1)}, u32[]{:S(2)}) copy-start(bf16[4,8,24,4096]{3,2,1,0:T(8,128)(2,1)} %get-tuple-element.9) | copy-start | bytes 18874372
  128.8 8.1 %copy-start.2 = (bf16[768,1792]{1,0:T(8,128)(2,1)}, bf16[768,1792]{1,0:T(8,128)(2,1)S(1)}, u32[]{:S(2)}) copy-start(bf16[768,1792]{1,0:T(8,128)(2,1)S(1)} %get-tuple-element.12) | copy-start | bytes 8257540
  137.0 6.5 %copy-start.3 = (bf16[768,1792]{1,0:T(8,128)(2,1)S(1)}, bf16[768,1792]{1,0:T(8,128)(2,1)}, u32[]{:S(2)}) copy-start(bf16[768,1792]{1,0:T(8,128)(2,1)} %get-tuple-element.11) | copy-start | bytes 8257540
